TPU v7x, 32 devices: a whole 2x2x4 slice. The times are simulated.
32 devices in a mesh: groups: 2 (over x), expert: 16 (over z, y, core).
Axes of the slice: x: 2, y: 2, z: 4, core: 2. Of those that a mesh axis runs over, the one named last changes fastest.
Arguments:
- query_features: bfloat16 [4096, 1024], P(('groups', 'expert')), parts along dimension 0, may hold values from -6 to 6
- query_job_label: int32 [4096], P(('groups', 'expert')), parts along dimension 0, may hold values from 0 to 7, as said below
- selected_specialists: int32 [4096, 2], P(('groups', 'expert')), parts along dimension 0, may hold values from 0 to 8, as said below
- whole_number_mixing_factors: int32 [4096, 2], P(('groups', 'expert')), parts along dimension 0, may hold values from 1 to 8
- copy_room_sizes: int32 [16], replicated, may hold values from 256 to 384, as said below
- first_layer_matrix: bfloat16 [16, 1024, 2048], P('expert'), as said below
- second_layer_matrix: bfloat16 [16, 2048, 1024], P('expert'), as said below
Outputs:
- mixture: bfloat16 [4096, 1024], P(('groups', 'expert')), parts along dimension 0
There are 2 independent parts, one for each index of `groups`. A program takes and returns all parts, laid end to end along the dimension named above; an argument that names none is the same for every part. Nothing has to cross between parts.
Inputs may be any that keep to these rules, and one draw needn't show every extreme that they name: `query_job_label`: each request's task number; column 0 of `selected_specialists` names a task expert of this task. `selected_specialists`: column 0 names a task expert of the row's task (number r from 8 on is task expert r - 8), column 1 a shared expert (below 8). From the rows of one device at most 32 entries go to one expert copy, and in every draw some copy receives exactly 32 entries from every device. `copy_room_sizes`: some copy has capacity 384 and some copy 2 * 128. `first_layer_matrix`: the 1 copies of one shared expert hold equal weights. `second_layer_matrix`: the 1 copies of one shared expert hold equal weights.
All inputs are finite; a program needn't handle non-finite values.
Results may differ from a plain program's by a relative error of at most 0.0058.
Values may be sent and summed in bfloat16 or wider, within the bound.
No kernel may reach another device: no remote copies, remote signals or barrier semaphores. Data moves between devices by JAX's collectives and lax.ppermute only.
A program may use at most 64 MiB of HBM per device.

v0:
```python
import jax
import jax.numpy as jnp
from jax import lax
from jax.sharding import PartitionSpec as P

TASKS = 8
SHARED = 8


def expert_mlp(block_rows, up_matrix, down_matrix):
    hidden = jax.nn.gelu(jnp.dot(block_rows, up_matrix, preferred_element_type=jnp.float32)).astype(
        jnp.bfloat16
    )
    return jnp.dot(hidden, down_matrix, preferred_element_type=jnp.float32).astype(jnp.bfloat16)


def shards(
    query_features,
    query_job_label,
    selected_specialists,
    whole_number_mixing_factors,
    copy_room_sizes,
    first_layer_matrix,
    second_layer_matrix,
):
    specialist_networks = copy_room_sizes.shape[0]
    row_count = query_features.shape[0]
    feature_width = query_features.shape[1]
    top_count = selected_specialists.shape[1]
    copies = specialist_networks // (2 * SHARED)
    task_width = specialist_networks // (2 * TASKS)
    slot_size = 4 * row_count // specialist_networks
    up_matrix = first_layer_matrix[0]
    down_matrix = second_layer_matrix[0]
    own_index = lax.axis_index("expert")
    row_local = jnp.arange(row_count, dtype=jnp.int32)
    shared_copy = selected_specialists * copies + (row_local % copies)[:, None]
    task_copy = (
        SHARED * copies + query_job_label[:, None] * task_width + selected_specialists - SHARED
    )
    expert_ids = jnp.where(selected_specialists < SHARED, shared_copy, task_copy)
    linear_specialist_number = expert_ids.reshape(-1)
    specialist_onehot = (
        linear_specialist_number[:, None]
        == jnp.arange(specialist_networks, dtype=jnp.int32)[None, :]
    ).astype(jnp.int32)
    counts = jnp.sum(specialist_onehot, axis=0)
    local_rank = jnp.sum(
        (jnp.cumsum(specialist_onehot, axis=0) - specialist_onehot) * specialist_onehot, axis=1
    )
    all_counts = lax.all_gather(counts[None, :], "expert", axis=0, tiled=True)
    below_mask = (jnp.arange(all_counts.shape[0]) < own_index).astype(jnp.int32)
    offset = jnp.sum(all_counts * below_mask[:, None], axis=0)
    arrival_rank = local_rank + jnp.sum(specialist_onehot * offset[None, :], axis=1)
    slot_room_bounds = jnp.sum(specialist_onehot * copy_room_sizes[None, :], axis=1)
    surviving_slot_flags = arrival_rank < slot_room_bounds
    source_rows = jnp.arange(linear_specialist_number.shape[0], dtype=jnp.int32) // top_count
    send_index = jnp.where(
        surviving_slot_flags,
        linear_specialist_number * slot_size + local_rank,
        specialist_networks * slot_size,
    )
    outgoing = jnp.zeros((specialist_networks * slot_size, feature_width), jnp.bfloat16)
    outgoing = (
        outgoing.at[send_index]
        .set(query_features[source_rows], mode="drop")
        .reshape(specialist_networks, slot_size, feature_width)
    )
    arrived = lax.all_to_all(outgoing, "expert", split_axis=0, concat_axis=0, tiled=True)
    returned = lax.all_to_all(
        expert_mlp(arrived.reshape(-1, feature_width), up_matrix, down_matrix).reshape(
            arrived.shape
        ),
        "expert",
        split_axis=0,
        concat_axis=0,
        tiled=True,
    )
    read_index = jnp.where(
        surviving_slot_flags, linear_specialist_number * slot_size + local_rank, 0
    )
    picked = returned.reshape(-1, feature_width)[read_index]
    gate_float = whole_number_mixing_factors.astype(jnp.float32)
    gate_share = gate_float / jnp.sum(gate_float, axis=1, keepdims=True)
    row_weight = gate_share.reshape(-1) * surviving_slot_flags.astype(jnp.float32)
    weighted = row_weight[:, None] * picked.astype(jnp.float32)
    return jnp.sum(weighted.reshape(row_count, top_count, feature_width), axis=1).astype(
        jnp.bfloat16
    )


def solution(mesh):
    in_specs = (
        P(("groups", "expert"), None),
        P(("groups", "expert")),
        P(("groups", "expert"), None),
        P(("groups", "expert"), None),
        P(),
        P("expert", None, None),
        P("expert", None, None),
    )
    out_specs = P(("groups", "expert"), None)
    return jax.shard_map(shards, mesh=mesh, in_specs=in_specs, out_specs=out_specs, check_vma=False)
```

profile of v0, /device:TPU:0, one launch (start us, length us, event | category | flops | bytes accessed | tf_op | source)
XLA Modules:
  0.0 91.7 jit_solution(5855867571831604541)
XLA Ops:
  0.0 0.7 broadcast_add_fusion
  0.7 0.7 broadcast_multiply_fusion
  1.4 0.1 copy.23
  1.5 0.1 eq.27
  1.6 0.1 eq.31
  1.8 0.1 convert_reduce_fusion
  1.9 1.2 %dynamic-slice = u32[1]{0:T(128)} dynamic-slice(u32[32]{0:T(128)} %constant.70, u32[]{:T(128)S(6)} %add.123), dynamic_slice_sizes={1} | dynamic-slice | bytes 12
  3.8 0.2 dynamic-update-slice
  4.1 13.8 %all-reduce = s32[256]{0:T(256)S(1)} all-reduce(s32[256]{0:T(256)S(1)} %dynamic-update-slice), channel_id=2, replica_groups=mesh['groups'=2,'expert'=16] {'expert'}, use_global_device_ids=true, to_apply=%add | all-reduce | flops 256 | bytes 2048
  17.9 0.6 reduce-window.6
  18.5 0.2 slice_reduce_fusion
  18.7 0.1 copy.28
  18.9 0.1 mul.88
  19.1 0.7 select_reduce_fusion.1
  19.9 3.7 %scatter_custom_fusion = bf16[512,1024]{1,0:T(8,128)(2,1)S(1)} fusion(s32[256]{0:T(256)S(1)} %bitcast.43, bf16[128,1024]{1,0:T(8,128)(2,1)S(1)} %copy-done, s32[1024]{0:T(1024)S(1)} %pad_clamp_fusion.1, bf16[]{:T(256)} %constant.56.clone.1), kind=kCustom, calls=%fused_computation.18 | custom fusion | bytes 1048578 | tf_op jit(solution)/shard_map/scatter | solution.py:66
  23.6 27.3 %all_to_all.10 = bf16[16,32,1024]{2,1,0:T(8,128)(2,1)S(1)} all-to-all(bf16[16,32,1024]{2,1,0:T(8,128)(2,1)S(1)} %bitcast.36), channel_id=1, replica_groups=mesh['groups'=2,'expert'=16] {'expert'}, dimensions={0} | all-to-all | bytes 2097152 | tf_op jit(solution)/shard_map/all_to_all | solution.py:69
  50.9 9.0 %fusion.14 = bf16[512,1024]{1,0:T(8,128)(2,1)} fusion(bf16[1,2048,1024]{2,1,0:T(8,128)(2,1)} %param.13, bf16[512,1024]{1,0:T(8,128)(2,1)S(1)} %bitcast.37, bf16[1,1024,2048]{2,1,0:T(8,128)(2,1)} %param.12), kind=kOutput, calls=%fused_computation.16 | convolution fusion | flops 4304928768 | bytes 10485760 | tf_op jit(solution)/shard_map/dot_general | solution.py:14
  59.9 4.9 %all-to-all-start.1 = ((bf16[16,32,1024]{2,1,0:T(8,128)(2,1)}), bf16[16,32,1024]{2,1,0:T(8,128)(2,1)S(1)}, u32[]{:S(2)}, u32[]{:S(2)}) async-start(bf16[16,32,1024]{2,1,0:T(8,128)(2,1)} %bitcast.11), calls=%async_computation.1 | async-start | bytes 2097152 | tf_op jit(solution)/shard_map/all_to_all | solution.py:70
  64.9 0.2 lt.73
  65.2 0.1 copy.27
  65.3 22.4 %all-to-all-done.1 = bf16[16,32,1024]{2,1,0:T(8,128)(2,1)S(1)} async-done(((bf16[16,32,1024]{2,1,0:T(8,128)(2,1)}), bf16[16,32,1024]{2,1,0:T(8,128)(2,1)S(1)}, u32[]{:S(2)}, u32[]{:S(2)}) %all-to-all-start.1) | async-done | bytes 1048608 | tf_op jit(solution)/shard_map/all_to_all | solution.py:70
  87.8 1.2 %gather_fusion = bf16[256,1024]{1,0:T(8,128)(2,1)S(1)} fusion(bf16[512,1024]{1,0:T(8,128)(2,1)S(1)} %bitcast.35, s32[1024]{0:T(1024)S(1)} %pad_clamp_fusion), kind=kCustom, calls=%fused_computation.1 | custom fusion | bytes 1049600 | tf_op jit(solution)/shard_map/gather | solution.py:82
  88.9 0.7 reshape.186
  89.6 2.1 %multiply_reduce_fusion = bf16[128,1024]{1,0:T(8,128)(2,1)} fusion(f32[128,2,1024]{2,1,0:T(2,128)S(1)} %reshape.186, f32[128,2]{1,0:T(8,128)S(1)} %copy.27), kind=kLoop, calls=%fused_computation.17 | loop fusion | flops 393216 | bytes 1311744 | tf_op jit(solution)/shard_map/reduce_sum | solution.py:87
  (19 shorter events, 0.4 us)
Async XLA Ops:
  0.0 19.9 %copy-start = (bf16[128,1024]{1,0:T(8,128)(2,1)S(1)}, bf16[128,1024]{1,0:T(8,128)(2,1)}, u32[]{:S(2)}) copy-start(bf16[128,1024]{1,0:T(8,128)(2,1)} %param.7) | copy-start | bytes 786436
  50.9 14.2 %copy-start.1 = (s32[128,2]{0,1:T(2,128)S(1)}, s32[128,2]{0,1:T(2,128)}, u32[]{:S(2)}) copy-start(s32[128,2]{0,1:T(2,128)} %param.10) | copy-start | bytes 3076
  59.9 27.8 %all-to-all-start.1 = ((bf16[16,32,1024]{2,1,0:T(8,128)(2,1)}), bf16[16,32,1024]{2,1,0:T(8,128)(2,1)S(1)}, u32[]{:S(2)}, u32[]{:S(2)}) async-start(bf16[16,32,1024]{2,1,0:T(8,128)(2,1)} %bitcast.11), calls=%async_computation.1 | async-start | bytes 2097152 | tf_op jit(solution)/shard_map/all_to_all | solution.py:70
where the time goes:
time: 93.1 us; the launch traced here: 91.7 us
  blocking collectives  41 us (44%)
  waiting for transfers between devices  22.4 us (24%)
  matrix products  9.05 us (10%)
  local copies, waits for them, and re-layouts  8.28 us (9%)
  other arithmetic  5.12 us (5%)
  starting transfers between devices  4.94 us (5%)
    all_to_all x1, blocking collectives, shards(): lax.all_to_all(outgoing, 'expert', split_axis=0, concat_axis=0, tiled=True)  27.3 us
    all_to_all x1, waiting for transfers between devices, shards(): lax.all_to_all(expert_mlp(arrived.reshape(-1, feature_width), up_matrix,...  22.4 us
    unnamed x1, blocking collectives  13.8 us
    dot_general x1, matrix products, expert_mlp(): jnp.dot(hidden, down_matrix, preferred_element_type=jnp.float32)  9.05 us
    all_to_all x1, starting transfers between devices, shards(): lax.all_to_all(expert_mlp(arrived.reshape(-1, feature_width), up_matrix,...  4.94 us
    scatter x1, local copies, waits for them, and re-layouts, shards(): outgoing = outgoing.at[send_index].set(query_features[source_rows], mode=...  3.71 us
    reduce_sum x1, other arithmetic, shards(): jnp.sum(weighted.reshape(row_count, top_count, feature_width), axis=1)  2.08 us
  transfers between devices with their start and end apart: 1, of which 1 were waited for; matrix products, arithmetic and copies ran while one was open for 0% of the time, Pallas kernels for 0%

commit v1 on v0

v1 whole, which is shorter than its diff:
```python
import jax
import jax.numpy as jnp
from jax import lax
from jax.sharding import PartitionSpec as P

SHARED = 8


def expert_mlp(block_rows, up_matrix, down_matrix):
    hidden = jax.nn.gelu(jnp.dot(block_rows, up_matrix, preferred_element_type=jnp.float32)).astype(
        jnp.bfloat16
    )
    return jnp.dot(hidden, down_matrix, preferred_element_type=jnp.float32)


def slots_of(ids, slot_size):
    count = ids.shape[0]
    row = lax.broadcasted_iota(jnp.int32, (count, count), 0)
    col = lax.broadcasted_iota(jnp.int32, (count, count), 1)
    before = (ids[:, None] == ids[None, :]) & (col < row)
    return ids * slot_size + jnp.sum(before.astype(jnp.int32), axis=1)


def counts_of(ids, half):
    experts = lax.broadcasted_iota(jnp.int32, (half, ids.shape[0]), 0)
    return jnp.sum((experts == ids[None, :]).astype(jnp.int32), axis=1)


def spread(rows, slots, slot_total):
    place = lax.broadcasted_iota(jnp.int32, (slot_total, rows.shape[0]), 0) == slots[None, :]
    return jnp.dot(place.astype(jnp.bfloat16), rows, preferred_element_type=jnp.float32).astype(
        jnp.bfloat16
    )


def pick(slot_rows, slots):
    place = (
        lax.broadcasted_iota(jnp.int32, (slots.shape[0], slot_rows.shape[0]), 1) == slots[:, None]
    )
    return jnp.dot(place.astype(jnp.bfloat16), slot_rows, preferred_element_type=jnp.float32)


def shards(
    query_features,
    query_job_label,
    selected_specialists,
    whole_number_mixing_factors,
    copy_room_sizes,
    first_layer_matrix,
    second_layer_matrix,
):
    experts = copy_room_sizes.shape[0]
    half = experts // 2
    row_count, width = query_features.shape
    copies = half // SHARED
    slot_size = 4 * row_count // experts
    slot_total = half * slot_size
    up_matrix = first_layer_matrix[0]
    down_matrix = second_layer_matrix[0]
    me = lax.axis_index("expert")
    upper = me >= half
    swap = [(i, (i + half) % experts) for i in range(experts)]
    halves = [list(range(half)), list(range(half, experts))]

    def exchange(array):
        return lax.all_to_all(
            array, "expert", split_axis=0, concat_axis=0, axis_index_groups=halves, tiled=True
        )

    task_id = query_job_label * copies + selected_specialists[:, 0] - SHARED
    row_local = jnp.arange(row_count, dtype=jnp.int32)
    shared_id = selected_specialists[:, 1] * copies + row_local % copies
    near_id = jnp.where(upper, task_id, shared_id)
    far_id = jnp.where(upper, shared_id, task_id)

    guest_rows = lax.ppermute(query_features, "expert", swap)
    guest_id = lax.ppermute(far_id, "expert", swap)

    near_slots = slots_of(near_id, slot_size)
    near_in = exchange(
        spread(query_features, near_slots, slot_total).reshape(half, slot_size, width)
    )
    guest_slots = slots_of(guest_id, slot_size)
    counts = exchange(
        jnp.stack([counts_of(near_id, half), counts_of(guest_id, half)], axis=1)
    )
    guest_in = exchange(spread(guest_rows, guest_slots, slot_total).reshape(half, slot_size, width))

    earlier = (
        lax.broadcasted_iota(jnp.int32, (half, half), 1)
        < lax.broadcasted_iota(jnp.int32, (half, half), 0)
    ).astype(jnp.int32)
    near_base = jnp.sum(earlier * counts[None, :, 0], axis=1) + jnp.where(
        upper, jnp.sum(counts[:, 1]), 0
    )
    guest_base = jnp.sum(earlier * counts[None, :, 1], axis=1) + jnp.where(
        upper, 0, jnp.sum(counts[:, 0])
    )
    room = copy_room_sizes[me]
    slot_local = jnp.arange(slot_size, dtype=jnp.int32)

    def serve(arrived, base):
        keep = (base[:, None] + slot_local[None, :] < room).reshape(-1, 1)
        result = expert_mlp(arrived.reshape(slot_total, width), up_matrix, down_matrix)
        kept = jnp.where(keep, result, 0.0).astype(jnp.bfloat16)
        return exchange(kept.reshape(half, slot_size, width)).reshape(slot_total, width)

    guest_out = pick(serve(guest_in, guest_base), guest_slots).astype(jnp.bfloat16)
    far_out = lax.ppermute(guest_out, "expert", swap).astype(jnp.float32)
    near_out = pick(serve(near_in, near_base), near_slots)

    gate_float = whole_number_mixing_factors.astype(jnp.float32)
    gate_share = gate_float / jnp.sum(gate_float, axis=1, keepdims=True)
    near_share = jnp.where(upper, gate_share[:, 0], gate_share[:, 1])
    far_share = jnp.where(upper, gate_share[:, 1], gate_share[:, 0])
    return (near_share[:, None] * near_out + far_share[:, None] * far_out).astype(jnp.bfloat16)


def solution(mesh):
    in_specs = (
        P(("groups", "expert"), None),
        P(("groups", "expert")),
        P(("groups", "expert"), None),
        P(("groups", "expert"), None),
        P(),
        P("expert", None, None),
        P("expert", None, None),
    )
    out_specs = P(("groups", "expert"), None)
    return jax.shard_map(shards, mesh=mesh, in_specs=in_specs, out_specs=out_specs, check_vma=False)
```

time: 93.1 us -> 77.9 us (0.84)
  blocking collectives: 41 us -> 0 us
  starting transfers between devices: 4.94 us -> 22.9 us
  matrix products: 9.05 us -> 18.1 us
  waiting for transfers between devices: 22.4 us -> 29 us
  local copies, waits for them, and re-layouts: 8.28 us -> 2.26 us
  other arithmetic: 5.12 us -> 3.7 us
    all_to_all x1 -> x0, blocking collectives: 27.3 us -> none  [shards(): lax.all_to_all(outgoing, 'expert', split_axis=0, concat_axis=0, tiled=True)]
    unnamed x1 -> x0, blocking collectives: 13.8 us -> none
    all_to_all x1 -> x5, starting transfers between devices: 4.94 us -> 18.1 us  [exchange(): lax.all_to_all(array, 'expert', split_axis=0, concat_axis=0, axis_index_g...]
    ppermute x0 -> x3, waiting for transfers between devices: none -> 9.89 us  [the longest x1 7.75 us: shards(): guest_rows = lax.ppermute(query_features, 'expert', swap)]
    dot_general x1 -> x6, matrix products: 9.05 us -> 18.1 us  [the longest x2 13.7 us: expert_mlp(): return jnp.dot(hidden, down_matrix, preferred_element_type=jnp.float32)]
    ppermute x0 -> x3, starting transfers between devices: none -> 4.84 us  [the longest x1 4.06 us: shards(): guest_id = lax.ppermute(far_id, 'expert', swap)]
    scatter x1 -> x0, local copies, waits for them, and re-layouts: 3.71 us -> none  [shards(): outgoing = outgoing.at[send_index].set(query_features[source_rows], mode=...]
    all_to_all x1 -> x5, waiting for transfers between devices: 22.4 us -> 19.1 us  [exchange(): lax.all_to_all(array, 'expert', split_axis=0, concat_axis=0, axis_index_g...]
  transfers between devices with their start and end apart: 1 -> 8, of which waited for: 1 -> 6; matrix products, arithmetic and copies ran while one was open for 0% -> 29% of each run, Pallas kernels for 0% -> 0%
where the time goes in v1:
time: 77.9 us; the launch traced here: 77.3 us
  waiting for transfers between devices  29 us (37%)
  starting transfers between devices  22.9 us (29%)
  matrix products  18.1 us (23%)
  other arithmetic  3.7 us (5%)
  local copies, waits for them, and re-layouts  2.26 us (3%)
  between operations  1.32 us (2%)
    all_to_all x5, waiting for transfers between devices, exchange(): lax.all_to_all(array, 'expert', split_axis=0, concat_axis=0, axis_index_g...  19.1 us
    all_to_all x5, starting transfers between devices, exchange(): lax.all_to_all(array, 'expert', split_axis=0, concat_axis=0, axis_index_g...  18.1 us
    dot_general x2, matrix products, expert_mlp(): return jnp.dot(hidden, down_matrix, preferred_element_type=jnp.float32)  13.7 us
    ppermute x1, waiting for transfers between devices, shards(): guest_rows = lax.ppermute(query_features, 'expert', swap)  7.75 us
    ppermute x1, starting transfers between devices, shards(): guest_id = lax.ppermute(far_id, 'expert', swap)  4.06 us
    dot_general x2, matrix products, spread(): jnp.dot(place.astype(jnp.bfloat16), rows, preferred_element_type=jnp.floa...  3.13 us
    ppermute x1, waiting for transfers between devices, shards(): far_out = lax.ppermute(guest_out, 'expert', swap).astype(jnp.float32)  2.14 us
  transfers between devices with their start and end apart: 8, of which 6 were waited for; matrix products, arithmetic and copies ran while one was open for 29% of the time, Pallas kernels for 0%

profile of v1, /device:TPU:0, one launch (start us, length us, event | category | flops | bytes accessed | tf_op | source)
XLA Modules:
  0.0 77.3 jit_solution(6096334998204134691)
XLA Ops:
  0.0 0.8 broadcast_select_fusion.1
  0.8 4.1 %collective-permute-start = (s32[128]{0:T(128)S(1)}, s32[128]{0:T(128)S(1)}, u32[]{:S(2)}, u32[]{:S(2)}) collective-permute-start(s32[128]{0:T(128)S(1)} %get-tuple-element.8), channel_id=1, source_target_pairs={{0,8},{1,9},{2,10},{3,11},{4,12},{5,13},{6,14},{7,15},{8,0},{9,1},... | collective-permute-start | bytes 1544 | tf_op jit(solution)/shard_map/ppermute | solution.py:77
  5.2 1.3 %dynamic_slice.3 = s32[1]{0:T(128)} dynamic-slice(s32[16]{0:T(128)} %param.11, s32[]{:T(128)S(6)} %select_n.56), dynamic_slice_sizes={1} | dynamic-slice | bytes 12 | tf_op jit(solution)/shard_map/dynamic_slice | solution.py:99
  6.6 0.7 copy.10
  7.3 4.1 %all-to-all-start = ((s32[8,1,2]{2,1,0:T(1,128)}), s32[8,1,2]{2,1,0:T(1,128)S(1)}, u32[]{:S(2)}, u32[]{:S(2)}) async-start(s32[8,1,2]{2,1,0:T(1,128)} %copy.10), calls=%async_computation | async-start | bytes 8192 | tf_op jit(solution)/shard_map/all_to_all | solution.py:66
  11.6 7.8 %collective-permute-done.1 = bf16[128,1024]{1,0:T(8,128)(2,1)S(1)} collective-permute-done((bf16[128,1024]{1,0:T(8,128)(2,1)}, bf16[128,1024]{1,0:T(8,128)(2,1)S(1)}, u32[]{:S(2)}, u32[]{:S(2)}) %collective-permute-start.1) | collective-permute-done | bytes 262176 | tf_op jit(solution)/shard_map/ppermute | solution.py:76
  19.3 1.1 %convolution_convert_fusion = bf16[256,1024]{1,0:T(8,128)(2,1)} fusion(bf16[128,1024]{1,0:T(8,128)(2,1)S(1)} %collective-permute-done.1, s32[128]{0:T(128)S(1)} %multiply_add_fusion), kind=kOutput, calls=%fused_computation.30 | convolution fusion | flops 67403776 | bytes 786944 | tf_op jit(solution)/shard_map/dot_general | solution.py:31
  20.4 3.5 %all-to-all-start.3 = ((bf16[8,32,1024]{2,1,0:T(8,128)(2,1)}), bf16[8,32,1024]{2,1,0:T(8,128)(2,1)S(1)}, u32[]{:S(2)}, u32[]{:S(2)}) async-start(bf16[8,32,1024]{2,1,0:T(8,128)(2,1)} %bitcast.17), calls=%async_computation.3 | async-start | bytes 1048576 | tf_op jit(solution)/shard_map/all_to_all | solution.py:66
  23.9 2.0 %convolution_convert_fusion.1 = bf16[256,1024]{1,0:T(8,128)(2,1)} fusion(bf16[128,1024]{1,0:T(8,128)(2,1)} %param.7, s32[128]{0:T(128)S(1)} %multiply_add_fusion.1), kind=kOutput, calls=%fused_computation.31 | convolution fusion | flops 67403776 | bytes 786944 | tf_op jit(solution)/shard_map/dot_general | solution.py:31
  26.1 0.6 slice_bitcast_fusion.1
  27.5 0.8 add_compare_fusion
  28.9 3.8 %all-to-all-done.3 = bf16[8,32,1024]{2,1,0:T(8,128)(2,1)S(1)} async-done(((bf16[8,32,1024]{2,1,0:T(8,128)(2,1)}), bf16[8,32,1024]{2,1,0:T(8,128)(2,1)S(1)}, u32[]{:S(2)}, u32[]{:S(2)}) %all-to-all-start.3) | async-done | bytes 524320 | tf_op jit(solution)/shard_map/all_to_all | solution.py:66
  32.7 3.5 %all-to-all-start.1 = ((bf16[8,32,1024]{2,1,0:T(8,128)(2,1)}), bf16[8,32,1024]{2,1,0:T(8,128)(2,1)S(1)}, u32[]{:S(2)}, u32[]{:S(2)}) async-start(bf16[8,32,1024]{2,1,0:T(8,128)(2,1)} %bitcast.9), calls=%async_computation.1 | async-start | bytes 1048576 | tf_op jit(solution)/shard_map/all_to_all | solution.py:66
  36.2 6.9 %fusion.38 = bf16[256,1024]{1,0:T(8,128)(2,1)} fusion(bf16[1,2048,1024]{2,1,0:T(8,128)(2,1)} %param.13, bf16[256,1024]{1,0:T(8,128)(2,1)S(1)} %bitcast.71, bf16[1,1024,2048]{2,1,0:T(8,128)(2,1)} %param.12, pred[256]{0:T(512)(128)(4,1)S(1)} %lt.49), kind=kOutput, calls=%fused_computation.28 | convolution fusion | flops 2152726528 | bytes 9437440 | tf_op jit(solution)/shard_map/dot_general | solution.py:13
  43.1 1.9 %all-to-all-done.1 = bf16[8,32,1024]{2,1,0:T(8,128)(2,1)S(1)} async-done(((bf16[8,32,1024]{2,1,0:T(8,128)(2,1)}), bf16[8,32,1024]{2,1,0:T(8,128)(2,1)S(1)}, u32[]{:S(2)}, u32[]{:S(2)}) %all-to-all-start.1) | async-done | bytes 524320 | tf_op jit(solution)/shard_map/all_to_all | solution.py:66
  45.0 3.5 %all-to-all-start.4 = ((bf16[8,32,1024]{2,1,0:T(8,128)(2,1)}), bf16[8,32,1024]{2,1,0:T(8,128)(2,1)S(1)}, u32[]{:S(2)}, u32[]{:S(2)}) async-start(bf16[8,32,1024]{2,1,0:T(8,128)(2,1)} %bitcast.19), calls=%async_computation.4 | async-start | bytes 1048576 | tf_op jit(solution)/shard_map/all_to_all | solution.py:66
  48.5 0.8 add_compare_fusion.1
  49.4 6.9 %fusion.41 = bf16[256,1024]{1,0:T(8,128)(2,1)} fusion(bf16[1,2048,1024]{2,1,0:T(8,128)(2,1)} %param.13, bf16[256,1024]{1,0:T(8,128)(2,1)S(1)} %bitcast.72, bf16[1,1024,2048]{2,1,0:T(8,128)(2,1)} %param.12, pred[256]{0:T(512)(128)(4,1)S(1)} %lt.47), kind=kOutput, calls=%fused_computation.29 | convolution fusion | flops 2152726528 | bytes 9437440 | tf_op jit(solution)/shard_map/dot_general | solution.py:13
  56.2 1.1 %all-to-all-done.4 = bf16[8,32,1024]{2,1,0:T(8,128)(2,1)S(1)} async-done(((bf16[8,32,1024]{2,1,0:T(8,128)(2,1)}), bf16[8,32,1024]{2,1,0:T(8,128)(2,1)S(1)}, u32[]{:S(2)}, u32[]{:S(2)}) %all-to-all-start.4) | async-done | bytes 524320 | tf_op jit(solution)/shard_map/all_to_all | solution.py:66
  57.3 3.5 %all-to-all-start.2 = ((bf16[8,32,1024]{2,1,0:T(8,128)(2,1)}), bf16[8,32,1024]{2,1,0:T(8,128)(2,1)S(1)}, u32[]{:S(2)}, u32[]{:S(2)}) async-start(bf16[8,32,1024]{2,1,0:T(8,128)(2,1)} %bitcast.13), calls=%async_computation.2 | async-start | bytes 1048576 | tf_op jit(solution)/shard_map/all_to_all | solution.py:66
  61.1 0.7 collective-permute-start.2
  61.8 12.4 %all-to-all-done.2 = bf16[8,32,1024]{2,1,0:T(8,128)(2,1)S(1)} async-done(((bf16[8,32,1024]{2,1,0:T(8,128)(2,1)}), bf16[8,32,1024]{2,1,0:T(8,128)(2,1)S(1)}, u32[]{:S(2)}, u32[]{:S(2)}) %all-to-all-start.2) | async-done | bytes 524320 | tf_op jit(solution)/shard_map/all_to_all | solution.py:66
  74.2 2.1 %collective-permute-done.2 = bf16[128,1024]{1,0:T(8,128)(2,1)S(1)} collective-permute-done((bf16[128,1024]{1,0:T(8,128)(2,1)S(1)}, bf16[128,1024]{1,0:T(8,128)(2,1)S(1)}, u32[]{:S(2)}, u32[]{:S(2)}) %collective-permute-start.2) | collective-permute-done | bytes 262176 | tf_op jit(solution)/shard_map/ppermute | solution.py:109
  76.3 1.0 %add_convert_fusion = bf16[128,1024]{1,0:T(8,128)(2,1)} fusion(bf16[128,1024]{1,0:T(8,128)(2,1)S(1)} %collective-permute-done.2, f32[128]{0:T(128)S(1)} %get-tuple-element.10, bf16[256,1024]{1,0:T(8,128)(2,1)S(1)} %bitcast.69, f32[128]{0:T(128)S(1)} %get-tuple-element.9, s32[128]{0:T(128)S(1)} %multiply_add_fusion.1), kind=kOutput, calls=%fused_computation.34 | convolution fusion | flops 67796992 | bytes 1050112 | tf_op jit(solution)/shard_map/dot_general | solution.py:40
  (22 shorter events, 1.4 us)
Async XLA Ops:
  0.8 5.8 %collective-permute-start = (s32[128]{0:T(128)S(1)}, s32[128]{0:T(128)S(1)}, u32[]{:S(2)}, u32[]{:S(2)}) collective-permute-start(s32[128]{0:T(128)S(1)} %get-tuple-element.8), channel_id=1, source_target_pairs={{0,8},{1,9},{2,10},{3,11},{4,12},{5,13},{6,14},{7,15},{8,0},{9,1},... | collective-permute-start | bytes 1544 | tf_op jit(solution)/shard_map/ppermute | solution.py:77
  4.8 14.5 %collective-permute-start.1 = (bf16[128,1024]{1,0:T(8,128)(2,1)}, bf16[128,1024]{1,0:T(8,128)(2,1)S(1)}, u32[]{:S(2)}, u32[]{:S(2)}) collective-permute-start(bf16[128,1024]{1,0:T(8,128)(2,1)} %param.7), channel_id=1, source_target_pairs={{0,8},{1,9},{2,10},{3,11},{4,12},{5,13},{6,14},{7,15},{8,0},{9,1},... | collective-permute-start | bytes 786440 | tf_op jit(solution)/shard_map/ppermute | solution.py:76
  7.3 13.1 %all-to-all-start = ((s32[8,1,2]{2,1,0:T(1,128)}), s32[8,1,2]{2,1,0:T(1,128)S(1)}, u32[]{:S(2)}, u32[]{:S(2)}) async-start(s32[8,1,2]{2,1,0:T(1,128)} %copy.10), calls=%async_computation | async-start | bytes 8192 | tf_op jit(solution)/shard_map/all_to_all | solution.py:66
  20.4 12.3 %all-to-all-start.3 = ((bf16[8,32,1024]{2,1,0:T(8,128)(2,1)}), bf16[8,32,1024]{2,1,0:T(8,128)(2,1)S(1)}, u32[]{:S(2)}, u32[]{:S(2)}) async-start(bf16[8,32,1024]{2,1,0:T(8,128)(2,1)} %bitcast.17), calls=%async_computation.3 | async-start | bytes 1048576 | tf_op jit(solution)/shard_map/all_to_all | solution.py:66
  32.7 12.3 %all-to-all-start.1 = ((bf16[8,32,1024]{2,1,0:T(8,128)(2,1)}), bf16[8,32,1024]{2,1,0:T(8,128)(2,1)S(1)}, u32[]{:S(2)}, u32[]{:S(2)}) async-start(bf16[8,32,1024]{2,1,0:T(8,128)(2,1)} %bitcast.9), calls=%async_computation.1 | async-start | bytes 1048576 | tf_op jit(solution)/shard_map/all_to_all | solution.py:66
  45.0 12.3 %all-to-all-start.4 = ((bf16[8,32,1024]{2,1,0:T(8,128)(2,1)}), bf16[8,32,1024]{2,1,0:T(8,128)(2,1)S(1)}, u32[]{:S(2)}, u32[]{:S(2)}) async-start(bf16[8,32,1024]{2,1,0:T(8,128)(2,1)} %bitcast.19), calls=%async_computation.4 | async-start | bytes 1048576 | tf_op jit(solution)/shard_map/all_to_all | solution.py:66
  49.4 11.4 %copy-start = (s32[128,2]{0,1:T(2,128)S(1)}, s32[128,2]{0,1:T(2,128)}, u32[]{:S(2)}) copy-start(s32[128,2]{0,1:T(2,128)} %param.10) | copy-start | bytes 3076
  57.3 16.9 %all-to-all-start.2 = ((bf16[8,32,1024]{2,1,0:T(8,128)(2,1)}), bf16[8,32,1024]{2,1,0:T(8,128)(2,1)S(1)}, u32[]{:S(2)}, u32[]{:S(2)}) async-start(bf16[8,32,1024]{2,1,0:T(8,128)(2,1)} %bitcast.13), calls=%async_computation.2 | async-start | bytes 1048576 | tf_op jit(solution)/shard_map/all_to_all | solution.py:66
  61.1 15.2 %collective-permute-start.2 = (bf16[128,1024]{1,0:T(8,128)(2,1)S(1)}, bf16[128,1024]{1,0:T(8,128)(2,1)S(1)}, u32[]{:S(2)}, u32[]{:S(2)}) collective-permute-start(bf16[128,1024]{1,0:T(8,128)(2,1)S(1)} %convolution_convert_fusion.2), channel_id=1, source_target_pairs={{0,8},{1,9},{2,10},{3,11},{4,12},{5,13},{6,14},{7,15},{8,0},{9,1},... | collective-permute-start | bytes 786440 | tf_op jit(solution)/shard_map/ppermute | solution.py:109

commit v2 on v1

--- a/solution.py
+++ b/solution.py
@@ -3,7 +3,9 @@
 from jax import lax
 from jax.sharding import PartitionSpec as P
 
+
 SHARED = 8
+EXTRA = 8
 
 
 def expert_mlp(block_rows, up_matrix, down_matrix):
@@ -76,15 +78,24 @@
     guest_rows = lax.ppermute(query_features, "expert", swap)
     guest_id = lax.ppermute(far_id, "expert", swap)
 
-    near_slots = slots_of(near_id, slot_size)
-    near_in = exchange(
-        spread(query_features, near_slots, slot_total).reshape(half, slot_size, width)
-    )
+    block = slot_size + EXTRA
+    near_slots = slots_of(near_id, block)
+    notes = jnp.stack([counts_of(near_id, half), counts_of(guest_id, half)], axis=1)
+    fill = jnp.pad(notes, ((0, 0), (slot_size, EXTRA - 2))).reshape(-1, 1).astype(jnp.float32)
+    place = lax.broadcasted_iota(jnp.int32, (half * block, row_count), 0) == near_slots[None, :]
+    near_out_blocks = (
+        jnp.dot(place.astype(jnp.bfloat16), query_features, preferred_element_type=jnp.float32)
+        + fill
+    ).astype(jnp.bfloat16)
+    near_blocks = exchange(near_out_blocks.reshape(half, block, width))
+    near_blocks, guest_rows = lax.optimization_barrier((near_blocks, guest_rows))
+
     guest_slots = slots_of(guest_id, slot_size)
-    counts = exchange(
-        jnp.stack([counts_of(near_id, half), counts_of(guest_id, half)], axis=1)
-    )
-    guest_in = exchange(spread(guest_rows, guest_slots, slot_total).reshape(half, slot_size, width))
+    guest_spread = spread(guest_rows, guest_slots, slot_total)
+    near_blocks, guest_spread = lax.optimization_barrier((near_blocks, guest_spread))
+    guest_in = exchange(guest_spread.reshape(half, slot_size, width))
+    near_in = near_blocks[:, :slot_size]
+    counts = jnp.max(near_blocks[:, slot_size:, :128].astype(jnp.float32), axis=2).astype(jnp.int32)
 
     earlier = (
         lax.broadcasted_iota(jnp.int32, (half, half), 1)
@@ -102,12 +113,16 @@
     def serve(arrived, base):
         keep = (base[:, None] + slot_local[None, :] < room).reshape(-1, 1)
         result = expert_mlp(arrived.reshape(slot_total, width), up_matrix, down_matrix)
-        kept = jnp.where(keep, result, 0.0).astype(jnp.bfloat16)
-        return exchange(kept.reshape(half, slot_size, width)).reshape(slot_total, width)
+        return jnp.where(keep, result, 0.0).astype(jnp.bfloat16)
 
-    guest_out = pick(serve(guest_in, guest_base), guest_slots).astype(jnp.bfloat16)
+    near_served = serve(near_in, near_base)
+    guest_served = serve(guest_in, guest_base)
+    guest_back = exchange(guest_served.reshape(half, slot_size, width))
+    guest_out = pick(guest_back.reshape(slot_total, width), guest_slots).astype(jnp.bfloat16)
+    near_served, guest_out = lax.optimization_barrier((near_served, guest_out))
     far_out = lax.ppermute(guest_out, "expert", swap).astype(jnp.float32)
-    near_out = pick(serve(near_in, near_base), near_slots)
+    near_back = exchange(near_served.reshape(half, slot_size, width))
+    near_out = pick(near_back.reshape(slot_total, width), near_slots // block * slot_size + near_slots % block)
 
     gate_float = whole_number_mixing_factors.astype(jnp.float32)
     gate_share = gate_float / jnp.sum(gate_float, axis=1, keepdims=True)
@@ -127,4 +142,5 @@
         P("expert", None, None),
     )
     out_specs = P(("groups", "expert"), None)
+
     return jax.shard_map(shards, mesh=mesh, in_specs=in_specs, out_specs=out_specs, check_vma=False)

time: 77.9 us -> 83.4 us (1.071)
  waiting for transfers between devices: 29 us -> 34.6 us
  local copies, waits for them, and re-layouts: 2.26 us -> 0.98 us
  starting transfers between devices: 22.9 us -> 23.8 us
    ppermute x1, waiting for transfers between devices: 2.14 us -> 14.1 us  [shards(): far_out = lax.ppermute(guest_out, 'expert', swap).astype(jnp.float32)]
    all_to_all x5 -> x4, waiting for transfers between devices: 19.1 us -> 8.82 us  [exchange(): lax.all_to_all(array, 'expert', split_axis=0, concat_axis=0, axis_index_g...]
    ppermute x1, waiting for transfers between devices: 7.75 us -> 10.4 us  [shards(): guest_rows = lax.ppermute(query_features, 'expert', swap)]
    ppermute x1, starting transfers between devices: 0.06 us -> 2.65 us  [shards(): guest_rows = lax.ppermute(query_features, 'expert', swap)]
    dot_general x0 -> x1, matrix products: none -> 2.12 us  [shards(): jnp.dot(place.astype(jnp.bfloat16), query_features, preferred_element_typ...]
    all_to_all x5 -> x4, starting transfers between devices: 18.1 us -> 16 us  [exchange(): lax.all_to_all(array, 'expert', split_axis=0, concat_axis=0, axis_index_g...]
    dot_general x2 -> x1, matrix products: 3.13 us -> 1.08 us  [spread(): jnp.dot(place.astype(jnp.bfloat16), rows, preferred_element_type=jnp.floa...]
    ppermute x1, waiting for transfers between devices: 0.01 us -> 1.23 us  [shards(): guest_id = lax.ppermute(far_id, 'expert', swap)]
  transfers between devices with their start and end apart: 8 -> 7, of which waited for: 6 -> 6; matrix products, arithmetic and copies ran while one was open for 29% -> 13% of each run, Pallas kernels for 0% -> 0%
where the time goes in v2:
time: 83.4 us; the launch traced here: 82.9 us
  waiting for transfers between devices  34.6 us (41%)
  starting transfers between devices  23.8 us (29%)
  matrix products  18.2 us (22%)
  other arithmetic  3.93 us (5%)
  between operations  1.44 us (2%)
  local copies, waits for them, and re-layouts  0.98 us (1%)
    all_to_all x4, starting transfers between devices, exchange(): lax.all_to_all(array, 'expert', split_axis=0, concat_axis=0, axis_index_g...  16 us
    ppermute x1, waiting for transfers between devices, shards(): far_out = lax.ppermute(guest_out, 'expert', swap).astype(jnp.float32)  14.1 us
    dot_general x2, matrix products, expert_mlp(): return jnp.dot(hidden, down_matrix, preferred_element_type=jnp.float32)  13.7 us
    ppermute x1, waiting for transfers between devices, shards(): guest_rows = lax.ppermute(query_features, 'expert', swap)  10.4 us
    all_to_all x4, waiting for transfers between devices, exchange(): lax.all_to_all(array, 'expert', split_axis=0, concat_axis=0, axis_index_g...  8.82 us
    ppermute x1, starting transfers between devices, shards(): guest_id = lax.ppermute(far_id, 'expert', swap)  4.06 us
    ppermute x1, starting transfers between devices, shards(): guest_rows = lax.ppermute(query_features, 'expert', swap)  2.65 us
    dot_general x1, matrix products, shards(): jnp.dot(place.astype(jnp.bfloat16), query_features, preferred_element_typ...  2.12 us
  transfers between devices with their start and end apart: 7, of which 6 were waited for; matrix products, arithmetic and copies ran while one was open for 13% of the time, Pallas kernels for 0%

profile of v2, /device:TPU:0, one launch (start us, length us, event | category | flops | bytes accessed | tf_op | source)
XLA Modules:
  0.0 82.9 jit_solution(11478057613591048633)
XLA Ops:
  0.0 0.8 broadcast_select_fusion.1
  0.8 4.1 %collective-permute-start = (s32[128]{0:T(128)S(1)}, s32[128]{0:T(128)S(1)}, u32[]{:S(2)}, u32[]{:S(2)}) collective-permute-start(s32[128]{0:T(128)S(1)} %get-tuple-element.24), channel_id=1, source_target_pairs={{0,8},{1,9},{2,10},{3,11},{4,12},{5,13},{6,14},{7,15},{8,0},{9,1},... | collective-permute-start | bytes 1544 | tf_op jit(solution)/shard_map/ppermute | solution.py:79
  5.1 1.2 %collective-permute-done = s32[128]{0:T(128)S(1)} collective-permute-done((s32[128]{0:T(128)S(1)}, s32[128]{0:T(128)S(1)}, u32[]{:S(2)}, u32[]{:S(2)}) %collective-permute-start) | collective-permute-done | bytes 544 | tf_op jit(solution)/shard_map/ppermute | solution.py:79
  6.7 2.1 %fusion.32 = bf16[320,1024]{1,0:T(8,128)(2,1)} fusion(bf16[128,1024]{1,0:T(8,128)(2,1)} %param.7, f32[320]{0:T(512)S(1)} %convert_element_type.67, s32[128]{0:T(128)S(1)} %get-tuple-element.22), kind=kOutput, calls=%fused_computation.27 | convolution fusion | flops 84582400 | bytes 919296 | tf_op jit(solution)/shard_map/dot_general | solution.py:87
  8.9 4.1 %all-to-all-start = ((bf16[8,40,1024]{2,1,0:T(8,128)(2,1)}), bf16[8,40,1024]{2,1,0:T(8,128)(2,1)S(1)}, u32[]{:S(2)}, u32[]{:S(2)}) async-start(bf16[8,40,1024]{2,1,0:T(8,128)(2,1)} %bitcast.5), calls=%async_computation | async-start | bytes 1310720 | tf_op jit(solution)/shard_map/all_to_all | solution.py:68
  13.0 2.7 %collective-permute-start.1 = (bf16[128,1024]{1,0:T(8,128)(2,1)S(1)}, bf16[128,1024]{1,0:T(8,128)(2,1)S(1)}, u32[]{:S(2)}, u32[]{:S(2)}) collective-permute-start(bf16[128,1024]{1,0:T(8,128)(2,1)S(1)} %copy-done), channel_id=1, source_target_pairs={{0,8},{1,9},{2,10},{3,11},{4,12},{5,13},{6,14},{7,15},{8,0},{9,1},... | collective-permute-start | bytes 786440 | tf_op jit(solution)/shard_map/ppermute | solution.py:78
  15.7 0.6 dynamic_slice.3
  16.5 10.4 %collective-permute-done.1 = bf16[128,1024]{1,0:T(8,128)(2,1)S(1)} collective-permute-done((bf16[128,1024]{1,0:T(8,128)(2,1)S(1)}, bf16[128,1024]{1,0:T(8,128)(2,1)S(1)}, u32[]{:S(2)}, u32[]{:S(2)}) %collective-permute-start.1) | collective-permute-done | bytes 262176 | tf_op jit(solution)/shard_map/ppermute | solution.py:78
  26.8 2.0 %all-to-all-done = bf16[8,40,1024]{2,1,0:T(8,128)(2,1)S(1)} async-done(((bf16[8,40,1024]{2,1,0:T(8,128)(2,1)}), bf16[8,40,1024]{2,1,0:T(8,128)(2,1)S(1)}, u32[]{:S(2)}, u32[]{:S(2)}) %all-to-all-start) | async-done | bytes 655392 | tf_op jit(solution)/shard_map/all_to_all | solution.py:68
  28.8 1.1 %convolution_convert_fusion = bf16[256,1024]{1,0:T(8,128)(2,1)} fusion(bf16[128,1024]{1,0:T(8,128)(2,1)S(1)} %collective-permute-done.1, s32[128]{0:T(128)S(1)} %multiply_add_fusion), kind=kOutput, calls=%fused_computation.32 | convolution fusion | flops 67403776 | bytes 786944 | tf_op jit(solution)/shard_map/dot_general | solution.py:33
  30.0 4.8 %all-to-all-start.1 = ((bf16[8,32,1024]{2,1,0:T(8,128)(2,1)}), bf16[8,32,1024]{2,1,0:T(8,128)(2,1)S(1)}, u32[]{:S(2)}, u32[]{:S(2)}) async-start(bf16[8,32,1024]{2,1,0:T(8,128)(2,1)} %bitcast.10), calls=%async_computation.1 | async-start | bytes 1048576 | tf_op jit(solution)/shard_map/all_to_all | solution.py:68
  34.9 0.8 slice_reduce_fusion.3
  37.2 0.7 add_compare_fusion
  38.0 5.7 %all-to-all-done.1 = bf16[8,32,1024]{2,1,0:T(8,128)(2,1)S(1)} async-done(((bf16[8,32,1024]{2,1,0:T(8,128)(2,1)}), bf16[8,32,1024]{2,1,0:T(8,128)(2,1)S(1)}, u32[]{:S(2)}, u32[]{:S(2)}) %all-to-all-start.1) | async-done | bytes 524320 | tf_op jit(solution)/shard_map/all_to_all | solution.py:68
  43.7 6.8 %fusion.39 = bf16[256,1024]{1,0:T(8,128)(2,1)} fusion(bf16[1,2048,1024]{2,1,0:T(8,128)(2,1)} %param.13, bf16[256,1024]{1,0:T(8,128)(2,1)S(1)} %bitcast.65, bf16[1,1024,2048]{2,1,0:T(8,128)(2,1)} %param.12, pred[256]{0:T(512)(128)(4,1)S(1)} %lt.54), kind=kOutput, calls=%fused_computation.30 | convolution fusion | flops 2152726528 | bytes 9437440 | tf_op jit(solution)/shard_map/dot_general | solution.py:15
  50.5 3.5 %all-to-all-start.2 = ((bf16[8,32,1024]{2,1,0:T(8,128)(2,1)}), bf16[8,32,1024]{2,1,0:T(8,128)(2,1)S(1)}, u32[]{:S(2)}, u32[]{:S(2)}) async-start(bf16[8,32,1024]{2,1,0:T(8,128)(2,1)} %bitcast.12), calls=%async_computation.2 | async-start | bytes 1048576 | tf_op jit(solution)/shard_map/all_to_all | solution.py:68
  54.0 0.7 add_compare_fusion.1
  54.8 6.9 %fusion.42 = bf16[256,1024]{1,0:T(8,128)(2,1)} fusion(bf16[1,2048,1024]{2,1,0:T(8,128)(2,1)} %param.13, bf16[256,1024]{1,0:T(8,128)(2,1)S(1)} %bitcast.64, bf16[1,1024,2048]{2,1,0:T(8,128)(2,1)} %param.12, pred[256]{0:T(512)(128)(4,1)S(1)} %lt.52), kind=kOutput, calls=%fused_computation.31 | convolution fusion | flops 2152726528 | bytes 9437440 | tf_op jit(solution)/shard_map/dot_general | solution.py:15
  61.7 1.1 %all-to-all-done.2 = bf16[8,32,1024]{2,1,0:T(8,128)(2,1)S(1)} async-done(((bf16[8,32,1024]{2,1,0:T(8,128)(2,1)}), bf16[8,32,1024]{2,1,0:T(8,128)(2,1)S(1)}, u32[]{:S(2)}, u32[]{:S(2)}) %all-to-all-start.2) | async-done | bytes 524320 | tf_op jit(solution)/shard_map/all_to_all | solution.py:68
  62.8 0.3 convolution_convert_fusion.1
  63.1 3.5 %all-to-all-start.3 = ((bf16[8,32,1024]{2,1,0:T(8,128)(2,1)}), bf16[8,32,1024]{2,1,0:T(8,128)(2,1)S(1)}, u32[]{:S(2)}, u32[]{:S(2)}) async-start(bf16[8,32,1024]{2,1,0:T(8,128)(2,1)} %bitcast.14), calls=%async_computation.3 | async-start | bytes 1048576 | tf_op jit(solution)/shard_map/all_to_all | solution.py:68
  66.6 1.1 %collective-permute-start.2 = (bf16[128,1024]{1,0:T(8,128)(2,1)S(1)}, bf16[128,1024]{1,0:T(8,128)(2,1)S(1)}, u32[]{:S(2)}, u32[]{:S(2)}) collective-permute-start(bf16[128,1024]{1,0:T(8,128)(2,1)S(1)} %convolution_convert_fusion.1), channel_id=1, source_target_pairs={{0,8},{1,9},{2,10},{3,11},{4,12},{5,13},{6,14},{7,15},{8,0},{9,1},... | collective-permute-start | bytes 786440 | tf_op jit(solution)/shard_map/ppermute | solution.py:123
  67.8 14.1 %collective-permute-done.2 = bf16[128,1024]{1,0:T(8,128)(2,1)S(1)} collective-permute-done((bf16[128,1024]{1,0:T(8,128)(2,1)S(1)}, bf16[128,1024]{1,0:T(8,128)(2,1)S(1)}, u32[]{:S(2)}, u32[]{:S(2)}) %collective-permute-start.2) | collective-permute-done | bytes 262176 | tf_op jit(solution)/shard_map/ppermute | solution.py:123
  81.9 1.0 %add_convert_fusion = bf16[128,1024]{1,0:T(8,128)(2,1)} fusion(bf16[128,1024]{1,0:T(8,128)(2,1)S(1)} %collective-permute-done.2, f32[128]{0:T(128)S(1)} %get-tuple-element.26, bf16[256,1024]{1,0:T(8,128)(2,1)S(1)} %bitcast.62, f32[128]{0:T(128)S(1)} %get-tuple-element.25, s32[128]{0:T(128)S(1)} %get-tuple-element.21), kind=kOutput, calls=%fused_computation.35 | convolution fusion | flops 67796992 | bytes 1050112 | tf_op jit(solution)/shard_map/dot_general | solution.py:42
  (28 shorter events, 1.4 us)
Async XLA Ops:
  0.0 13.0 %copy-start = (bf16[128,1024]{1,0:T(8,128)(2,1)S(1)}, bf16[128,1024]{1,0:T(8,128)(2,1)}, u32[]{:S(2)}) copy-start(bf16[128,1024]{1,0:T(8,128)(2,1)} %param.7) | copy-start | bytes 786436
  0.0 15.7 %copy-start.2 = (s32[16]{0:T(128)S(1)}, s32[16]{0:T(128)}, u32[]{:S(2)}) copy-start(s32[16]{0:T(128)} %param.11) | copy-start | bytes 196
  0.8 5.6 %collective-permute-start = (s32[128]{0:T(128)S(1)}, s32[128]{0:T(128)S(1)}, u32[]{:S(2)}, u32[]{:S(2)}) collective-permute-start(s32[128]{0:T(128)S(1)} %get-tuple-element.24), channel_id=1, source_target_pairs={{0,8},{1,9},{2,10},{3,11},{4,12},{5,13},{6,14},{7,15},{8,0},{9,1},... | collective-permute-start | bytes 1544 | tf_op jit(solution)/shard_map/ppermute | solution.py:79
  8.9 20.0 %all-to-all-start = ((bf16[8,40,1024]{2,1,0:T(8,128)(2,1)}), bf16[8,40,1024]{2,1,0:T(8,128)(2,1)S(1)}, u32[]{:S(2)}, u32[]{:S(2)}) async-start(bf16[8,40,1024]{2,1,0:T(8,128)(2,1)} %bitcast.5), calls=%async_computation | async-start | bytes 1310720 | tf_op jit(solution)/shard_map/all_to_all | solution.py:68
  13.0 13.8 %collective-permute-start.1 = (bf16[128,1024]{1,0:T(8,128)(2,1)S(1)}, bf16[128,1024]{1,0:T(8,128)(2,1)S(1)}, u32[]{:S(2)}, u32[]{:S(2)}) collective-permute-start(bf16[128,1024]{1,0:T(8,128)(2,1)S(1)} %copy-done), channel_id=1, source_target_pairs={{0,8},{1,9},{2,10},{3,11},{4,12},{5,13},{6,14},{7,15},{8,0},{9,1},... | collective-permute-start | bytes 786440 | tf_op jit(solution)/shard_map/ppermute | solution.py:78
  30.0 13.7 %all-to-all-start.1 = ((bf16[8,32,1024]{2,1,0:T(8,128)(2,1)}), bf16[8,32,1024]{2,1,0:T(8,128)(2,1)S(1)}, u32[]{:S(2)}, u32[]{:S(2)}) async-start(bf16[8,32,1024]{2,1,0:T(8,128)(2,1)} %bitcast.10), calls=%async_computation.1 | async-start | bytes 1048576 | tf_op jit(solution)/shard_map/all_to_all | solution.py:68
  50.5 12.3 %all-to-all-start.2 = ((bf16[8,32,1024]{2,1,0:T(8,128)(2,1)}), bf16[8,32,1024]{2,1,0:T(8,128)(2,1)S(1)}, u32[]{:S(2)}, u32[]{:S(2)}) async-start(bf16[8,32,1024]{2,1,0:T(8,128)(2,1)} %bitcast.12), calls=%async_computation.2 | async-start | bytes 1048576 | tf_op jit(solution)/shard_map/all_to_all | solution.py:68
  54.8 11.8 %copy-start.1 = (s32[128,2]{0,1:T(2,128)S(1)}, s32[128,2]{0,1:T(2,128)}, u32[]{:S(2)}) copy-start(s32[128,2]{0,1:T(2,128)} %param.10) | copy-start | bytes 3076
  63.1 18.8 %all-to-all-start.3 = ((bf16[8,32,1024]{2,1,0:T(8,128)(2,1)}), bf16[8,32,1024]{2,1,0:T(8,128)(2,1)S(1)}, u32[]{:S(2)}, u32[]{:S(2)}) async-start(bf16[8,32,1024]{2,1,0:T(8,128)(2,1)} %bitcast.14), calls=%async_computation.3 | async-start | bytes 1048576 | tf_op jit(solution)/shard_map/all_to_all | solution.py:68
  66.6 15.2 %collective-permute-start.2 = (bf16[128,1024]{1,0:T(8,128)(2,1)S(1)}, bf16[128,1024]{1,0:T(8,128)(2,1)S(1)}, u32[]{:S(2)}, u32[]{:S(2)}) collective-permute-start(bf16[128,1024]{1,0:T(8,128)(2,1)S(1)} %convolution_convert_fusion.1), channel_id=1, source_target_pairs={{0,8},{1,9},{2,10},{3,11},{4,12},{5,13},{6,14},{7,15},{8,0},{9,1},... | collective-permute-start | bytes 786440 | tf_op jit(solution)/shard_map/ppermute | solution.py:123

commit v3 on v2

--- a/solution.py
+++ b/solution.py
@@ -116,19 +116,20 @@
         return jnp.where(keep, result, 0.0).astype(jnp.bfloat16)
 
     near_served = serve(near_in, near_base)
+    sent = jnp.concatenate([near_served, near_served], axis=0)
+    sent, guest_in = lax.optimization_barrier((sent, guest_in))
     guest_served = serve(guest_in, guest_base)
-    guest_back = exchange(guest_served.reshape(half, slot_size, width))
-    guest_out = pick(guest_back.reshape(slot_total, width), guest_slots).astype(jnp.bfloat16)
-    near_served, guest_out = lax.optimization_barrier((near_served, guest_out))
-    far_out = lax.ppermute(guest_out, "expert", swap).astype(jnp.float32)
-    near_back = exchange(near_served.reshape(half, slot_size, width))
-    near_out = pick(near_back.reshape(slot_total, width), near_slots // block * slot_size + near_slots % block)
+    start = jnp.where(upper, 0, slot_total)
+    sent = lax.dynamic_update_slice(sent, guest_served, (start, jnp.zeros_like(start)))
+    returned = lax.all_to_all(
+        sent.reshape(experts, slot_size, width), "expert", split_axis=0, concat_axis=0, tiled=True
+    ).reshape(experts * slot_size, width)
 
     gate_float = whole_number_mixing_factors.astype(jnp.float32)
     gate_share = gate_float / jnp.sum(gate_float, axis=1, keepdims=True)
-    near_share = jnp.where(upper, gate_share[:, 0], gate_share[:, 1])
-    far_share = jnp.where(upper, gate_share[:, 1], gate_share[:, 0])
-    return (near_share[:, None] * near_out + far_share[:, None] * far_out).astype(jnp.bfloat16)
+    task_out = pick(returned, slots_of(half + task_id, slot_size))
+    shared_out = pick(returned, slots_of(shared_id, slot_size))
+    return (gate_share[:, :1] * task_out + gate_share[:, 1:] * shared_out).astype(jnp.bfloat16)
 
 
 def solution(mesh):

time: 83.4 us -> 84.5 us (1.013); the launches traced: 82.9 us -> 82.9 us
  starting transfers between devices: 23.8 us -> 20.6 us
  other arithmetic: 3.93 us -> 6.04 us
  waiting for transfers between devices: 34.6 us -> 36.3 us
    all_to_all x0 -> x1, waiting for transfers between devices: none -> 22.6 us  [shards(): lax.all_to_all(sent.reshape(experts, slot_size, width), 'expert', split_a...]
    ppermute x1 -> x0, waiting for transfers between devices: 14.1 us -> none  [shards(): far_out = lax.ppermute(guest_out, 'expert', swap).astype(jnp.float32)]
    all_to_all x4 -> x2, starting transfers between devices: 16 us -> 8.97 us  [exchange(): lax.all_to_all(array, 'expert', split_axis=0, concat_axis=0, axis_index_g...]
    all_to_all x4 -> x2, waiting for transfers between devices: 8.82 us -> 2 us  [exchange(): lax.all_to_all(array, 'expert', split_axis=0, concat_axis=0, axis_index_g...]
    all_to_all x0 -> x1, starting transfers between devices: none -> 4.89 us  [shards(): lax.all_to_all(sent.reshape(experts, slot_size, width), 'expert', split_a...]
    concatenate x0 -> x1, other arithmetic: none -> 1.12 us  [shards(): sent = jnp.concatenate([near_served, near_served], axis=0)]
    ppermute x1 -> x0, starting transfers between devices: 1.1 us -> none  [shards(): far_out = lax.ppermute(guest_out, 'expert', swap).astype(jnp.float32)]
  transfers between devices with their start and end apart: 7 -> 5, of which waited for: 6 -> 4; matrix products, arithmetic and copies ran while one was open for 13% -> 12% of each run, Pallas kernels for 0% -> 0%
where the time goes in v3:
time: 84.5 us; the launch traced here: 82.9 us
  waiting for transfers between devices  36.3 us (43%)
  starting transfers between devices  20.6 us (24%)
  matrix products  17.6 us (21%)
  other arithmetic  6.04 us (7%)
  between operations  1.4 us (2%)
  local copies, waits for them, and re-layouts  0.98 us (1%)
    all_to_all x1, waiting for transfers between devices, shards(): lax.all_to_all(sent.reshape(experts, slot_size, width), 'expert', split_a...  22.6 us
    dot_general x2, matrix products, expert_mlp(): return jnp.dot(hidden, down_matrix, preferred_element_type=jnp.float32)  13 us
    ppermute x1, waiting for transfers between devices, shards(): guest_rows = lax.ppermute(query_features, 'expert', swap)  10.4 us
    all_to_all x2, starting transfers between devices, exchange(): lax.all_to_all(array, 'expert', split_axis=0, concat_axis=0, axis_index_g...  8.97 us
    all_to_all x1, starting transfers between devices, shards(): lax.all_to_all(sent.reshape(experts, slot_size, width), 'expert', split_a...  4.89 us
    ppermute x1, starting transfers between devices, shards(): guest_id = lax.ppermute(far_id, 'expert', swap)  4.06 us
    ppermute x1, starting transfers between devices, shards(): guest_rows = lax.ppermute(query_features, 'expert', swap)  2.65 us
    dot_general x1, matrix products, shards(): jnp.dot(place.astype(jnp.bfloat16), query_features, preferred_element_typ...  2.12 us
  transfers between devices with their start and end apart: 5, of which 4 were waited for; matrix products, arithmetic and copies ran while one was open for 12% of the time, Pallas kernels for 0%

profile of v3, /device:TPU:0, one launch (start us, length us, event | category | flops | bytes accessed | tf_op | source)
XLA Modules:
  0.0 82.9 jit_solution(9469749922210348082)
XLA Ops:
  0.0 0.8 broadcast_select_fusion.1
  0.8 0.2 convert_reduce_fusion.3
  0.9 0.7 multiply_add_fusion.2
  1.6 4.1 %collective-permute-start = (s32[128]{0:T(128)S(1)}, s32[128]{0:T(128)S(1)}, u32[]{:S(2)}, u32[]{:S(2)}) collective-permute-start(s32[128]{0:T(128)S(1)} %get-tuple-element.26), channel_id=1, source_target_pairs={{0,8},{1,9},{2,10},{3,11},{4,12},{5,13},{6,14},{7,15},{8,0},{9,1},... | collective-permute-start | bytes 1544 | tf_op jit(solution)/shard_map/ppermute | solution.py:79
  6.0 1.2 %collective-permute-done = s32[128]{0:T(128)S(1)} collective-permute-done((s32[128]{0:T(128)S(1)}, s32[128]{0:T(128)S(1)}, u32[]{:S(2)}, u32[]{:S(2)}) %collective-permute-start) | collective-permute-done | bytes 544 | tf_op jit(solution)/shard_map/ppermute | solution.py:79
  7.6 2.1 %fusion.32 = bf16[320,1024]{1,0:T(8,128)(2,1)} fusion(bf16[128,1024]{1,0:T(8,128)(2,1)} %param.7, f32[320]{0:T(512)S(1)} %convert_element_type.68, s32[128]{0:T(128)S(1)} %multiply_add_fusion.1), kind=kOutput, calls=%fused_computation.27 | convolution fusion | flops 84582400 | bytes 919296 | tf_op jit(solution)/shard_map/dot_general | solution.py:87
  9.7 4.1 %all-to-all-start = ((bf16[8,40,1024]{2,1,0:T(8,128)(2,1)}), bf16[8,40,1024]{2,1,0:T(8,128)(2,1)S(1)}, u32[]{:S(2)}, u32[]{:S(2)}) async-start(bf16[8,40,1024]{2,1,0:T(8,128)(2,1)} %bitcast.5), calls=%async_computation | async-start | bytes 1310720 | tf_op jit(solution)/shard_map/all_to_all | solution.py:68
  13.9 2.7 %collective-permute-start.1 = (bf16[128,1024]{1,0:T(8,128)(2,1)S(1)}, bf16[128,1024]{1,0:T(8,128)(2,1)S(1)}, u32[]{:S(2)}, u32[]{:S(2)}) collective-permute-start(bf16[128,1024]{1,0:T(8,128)(2,1)S(1)} %copy-done), channel_id=1, source_target_pairs={{0,8},{1,9},{2,10},{3,11},{4,12},{5,13},{6,14},{7,15},{8,0},{9,1},... | collective-permute-start | bytes 786440 | tf_op jit(solution)/shard_map/ppermute | solution.py:78
  16.5 0.6 dynamic_slice.3
  17.3 10.4 %collective-permute-done.1 = bf16[128,1024]{1,0:T(8,128)(2,1)S(1)} collective-permute-done((bf16[128,1024]{1,0:T(8,128)(2,1)S(1)}, bf16[128,1024]{1,0:T(8,128)(2,1)S(1)}, u32[]{:S(2)}, u32[]{:S(2)}) %collective-permute-start.1) | collective-permute-done | bytes 262176 | tf_op jit(solution)/shard_map/ppermute | solution.py:78
  27.7 2.0 %all-to-all-done = bf16[8,40,1024]{2,1,0:T(8,128)(2,1)S(1)} async-done(((bf16[8,40,1024]{2,1,0:T(8,128)(2,1)}), bf16[8,40,1024]{2,1,0:T(8,128)(2,1)S(1)}, u32[]{:S(2)}, u32[]{:S(2)}) %all-to-all-start) | async-done | bytes 655392 | tf_op jit(solution)/shard_map/all_to_all | solution.py:68
  29.7 1.1 %convolution_convert_fusion = bf16[256,1024]{1,0:T(8,128)(2,1)} fusion(bf16[128,1024]{1,0:T(8,128)(2,1)S(1)} %collective-permute-done.1, s32[128]{0:T(128)S(1)} %multiply_add_fusion), kind=kOutput, calls=%fused_computation.33 | convolution fusion | flops 67403776 | bytes 786944 | tf_op jit(solution)/shard_map/dot_general | solution.py:33
  30.9 0.7 slice_reduce_fusion.3
  32.2 4.8 %all-to-all-start.1 = ((bf16[8,32,1024]{2,1,0:T(8,128)(2,1)}), bf16[8,32,1024]{2,1,0:T(8,128)(2,1)S(1)}, u32[]{:S(2)}, u32[]{:S(2)}) async-start(bf16[8,32,1024]{2,1,0:T(8,128)(2,1)} %bitcast.10), calls=%async_computation.1 | async-start | bytes 1048576 | tf_op jit(solution)/shard_map/all_to_all | solution.py:68
  37.9 0.7 add_compare_fusion.1
  38.6 0.7 add_compare_fusion
  39.6 6.1 %fusion.45 = bf16[256,1024]{1,0:T(8,128)(2,1)S(1)} fusion(bf16[1,2048,1024]{2,1,0:T(8,128)(2,1)} %param.13, bf16[256,1024]{1,0:T(8,128)(2,1)S(1)} %bitcast.69, bf16[1,1024,2048]{2,1,0:T(8,128)(2,1)} %param.12, pred[256]{0:T(512)(128)(4,1)S(1)} %lt.54), kind=kOutput, calls=%fused_computation.32 | convolution fusion | flops 2152726528 | bytes 9437440 | tf_op jit(solution)/shard_map/dot_general | solution.py:15
  45.7 1.1 %pad_maximum_fusion = bf16[512,1024]{1,0:T(8,128)(2,1)} fusion(bf16[256,1024]{1,0:T(8,128)(2,1)S(1)} %fusion.45), kind=kLoop, calls=%fused_computation.38 | loop fusion | flops 2097152 | bytes 1572864 | tf_op jit(solution)/shard_map/concatenate | solution.py:119
  46.8 6.9 %fusion.42 = bf16[512,1024]{1,0:T(8,128)(2,1)} fusion(bf16[512,1024]{1,0:T(8,128)(2,1)} %pad_maximum_fusion, s32[]{:T(128)S(6)} %select_n.55, bf16[1,2048,1024]{2,1,0:T(8,128)(2,1)} %param.13, bf16[256,1024]{1,0:T(8,128)(2,1)S(1)} %bitcast.68, bf16[1,1024,2048]{2,1,0:T(8,128)(2,1)} %param.12, pred[256]{0:T(512)(128)(4,1)S(1)} %lt.56), kind=kOutput, calls=%fused_computation.31 | convolution fusion | flops 2152726528 | bytes 9437444 | tf_op jit(solution)/shard_map/dot_general | solution.py:15
  53.7 4.9 %all-to-all-start.2 = ((bf16[16,32,1024]{2,1,0:T(8,128)(2,1)}), bf16[16,32,1024]{2,1,0:T(8,128)(2,1)S(1)}, u32[]{:S(2)}, u32[]{:S(2)}) async-start(bf16[16,32,1024]{2,1,0:T(8,128)(2,1)} %bitcast.12), calls=%async_computation.2 | async-start | bytes 2097152 | tf_op jit(solution)/shard_map/all_to_all | solution.py:124
  58.6 0.2 convert_reduce_fusion
  58.8 22.6 %all-to-all-done.2 = bf16[16,32,1024]{2,1,0:T(8,128)(2,1)S(1)} async-done(((bf16[16,32,1024]{2,1,0:T(8,128)(2,1)}), bf16[16,32,1024]{2,1,0:T(8,128)(2,1)S(1)}, u32[]{:S(2)}, u32[]{:S(2)}) %all-to-all-start.2) | async-done | bytes 1048608 | tf_op jit(solution)/shard_map/all_to_all | solution.py:124
  81.5 0.4 convolution_multiply_fusion.1
  81.8 1.1 %fusion.49 = bf16[128,1024]{1,0:T(8,128)(2,1)} fusion(f32[128,1024]{1,0:T(8,128)S(1)} %convolution_multiply_fusion.1, bf16[512,1024]{1,0:T(8,128)(2,1)S(1)} %bitcast.67, f32[128]{0:T(128)S(1)} %get-tuple-element.23, s32[128]{0:T(128)S(1)} %fusion.62), kind=kOutput, calls=%fused_computation.37 | convolution fusion | flops 134676480 | bytes 1836032 | tf_op jit(solution)/shard_map/dot_general | solution.py:42
  (32 shorter events, 1.3 us)
Async XLA Ops:
  0.0 13.9 %copy-start = (bf16[128,1024]{1,0:T(8,128)(2,1)S(1)}, bf16[128,1024]{1,0:T(8,128)(2,1)}, u32[]{:S(2)}) copy-start(bf16[128,1024]{1,0:T(8,128)(2,1)} %param.7) | copy-start | bytes 786436
  0.0 16.5 %copy-start.3 = (s32[16]{0:T(128)S(1)}, s32[16]{0:T(128)}, u32[]{:S(2)}) copy-start(s32[16]{0:T(128)} %param.11) | copy-start | bytes 196
  1.6 5.6 %collective-permute-start = (s32[128]{0:T(128)S(1)}, s32[128]{0:T(128)S(1)}, u32[]{:S(2)}, u32[]{:S(2)}) collective-permute-start(s32[128]{0:T(128)S(1)} %get-tuple-element.26), channel_id=1, source_target_pairs={{0,8},{1,9},{2,10},{3,11},{4,12},{5,13},{6,14},{7,15},{8,0},{9,1},... | collective-permute-start | bytes 1544 | tf_op jit(solution)/shard_map/ppermute | solution.py:79
  9.7 20.0 %all-to-all-start = ((bf16[8,40,1024]{2,1,0:T(8,128)(2,1)}), bf16[8,40,1024]{2,1,0:T(8,128)(2,1)S(1)}, u32[]{:S(2)}, u32[]{:S(2)}) async-start(bf16[8,40,1024]{2,1,0:T(8,128)(2,1)} %bitcast.5), calls=%async_computation | async-start | bytes 1310720 | tf_op jit(solution)/shard_map/all_to_all | solution.py:68
  13.9 13.8 %collective-permute-start.1 = (bf16[128,1024]{1,0:T(8,128)(2,1)S(1)}, bf16[128,1024]{1,0:T(8,128)(2,1)S(1)}, u32[]{:S(2)}, u32[]{:S(2)}) collective-permute-start(bf16[128,1024]{1,0:T(8,128)(2,1)S(1)} %copy-done), channel_id=1, source_target_pairs={{0,8},{1,9},{2,10},{3,11},{4,12},{5,13},{6,14},{7,15},{8,0},{9,1},... | collective-permute-start | bytes 786440 | tf_op jit(solution)/shard_map/ppermute | solution.py:78
  32.2 14.6 %all-to-all-start.1 = ((bf16[8,32,1024]{2,1,0:T(8,128)(2,1)}), bf16[8,32,1024]{2,1,0:T(8,128)(2,1)S(1)}, u32[]{:S(2)}, u32[]{:S(2)}) async-start(bf16[8,32,1024]{2,1,0:T(8,128)(2,1)} %bitcast.10), calls=%async_computation.1 | async-start | bytes 1048576 | tf_op jit(solution)/shard_map/all_to_all | solution.py:68
  53.7 4.9 %copy-start.2 = (s32[128,2]{0,1:T(2,128)S(1)}, s32[128,2]{0,1:T(2,128)}, u32[]{:S(2)}) copy-start(s32[128,2]{0,1:T(2,128)} %param.10) | copy-start | bytes 3076
  53.7 4.9 %copy-start.1 = (s32[128,2]{0,1:T(2,128)S(1)}, s32[128,2]{0,1:T(2,128)}, u32[]{:S(2)}) copy-start(s32[128,2]{0,1:T(2,128)} %param.9) | copy-start | bytes 3076
  53.7 27.8 %all-to-all-start.2 = ((bf16[16,32,1024]{2,1,0:T(8,128)(2,1)}), bf16[16,32,1024]{2,1,0:T(8,128)(2,1)S(1)}, u32[]{:S(2)}, u32[]{:S(2)}) async-start(bf16[16,32,1024]{2,1,0:T(8,128)(2,1)} %bitcast.12), calls=%async_computation.2 | async-start | bytes 2097152 | tf_op jit(solution)/shard_map/all_to_all | solution.py:124

commit v4 on v1

v4 whole, which is shorter than its diff:
```python
import jax
import jax.numpy as jnp
from jax import lax
from jax.sharding import PartitionSpec as P

SHARED = 8
EMPTY = 64.0


def expert_mlp(block_rows, up_matrix, down_matrix):
    hidden = jax.nn.gelu(jnp.dot(block_rows, up_matrix, preferred_element_type=jnp.float32)).astype(
        jnp.bfloat16
    )
    return jnp.dot(hidden, down_matrix, preferred_element_type=jnp.float32)


def slots_of(ids, slot_size):
    count = ids.shape[0]
    row = lax.broadcasted_iota(jnp.int32, (count, count), 0)
    col = lax.broadcasted_iota(jnp.int32, (count, count), 1)
    before = (ids[:, None] == ids[None, :]) & (col < row)
    return ids * slot_size + jnp.sum(before.astype(jnp.int32), axis=1)


def pick(slot_rows, slots):
    place = (
        lax.broadcasted_iota(jnp.int32, (slots.shape[0], slot_rows.shape[0]), 1) == slots[:, None]
    )
    return jnp.dot(place.astype(jnp.bfloat16), slot_rows, preferred_element_type=jnp.float32)


def shards(
    query_features,
    query_job_label,
    selected_specialists,
    whole_number_mixing_factors,
    copy_room_sizes,
    first_layer_matrix,
    second_layer_matrix,
):
    experts = copy_room_sizes.shape[0]
    half = experts // 2
    row_count, width = query_features.shape
    copies = half // SHARED
    slot_size = 4 * row_count // experts
    slot_total = experts * slot_size
    me = lax.axis_index("expert")

    task_id = half + query_job_label * copies + selected_specialists[:, 0] - SHARED
    row_local = jnp.arange(row_count, dtype=jnp.int32)
    shared_id = selected_specialists[:, 1] * copies + row_local % copies
    task_slots = slots_of(task_id, slot_size)
    shared_slots = slots_of(shared_id, slot_size)

    slot = lax.broadcasted_iota(jnp.int32, (slot_total, row_count), 0)
    place = (slot == task_slots[None, :]) | (slot == shared_slots[None, :])
    fill = EMPTY - EMPTY * jnp.sum(place.astype(jnp.float32), axis=1, keepdims=True)
    placed = jnp.dot(place.astype(jnp.bfloat16), query_features, preferred_element_type=jnp.float32)
    sent = (placed + fill).astype(jnp.bfloat16)
    arrived = lax.all_to_all(
        sent.reshape(experts, slot_size, width), "expert", split_axis=0, concat_axis=0, tiled=True
    )

    level = jnp.max(arrived[:, :, :128].astype(jnp.float32), axis=2)
    counts = jnp.sum((level < EMPTY / 2).astype(jnp.int32), axis=1)
    earlier = (
        lax.broadcasted_iota(jnp.int32, (experts, experts), 1)
        < lax.broadcasted_iota(jnp.int32, (experts, experts), 0)
    ).astype(jnp.int32)
    base = jnp.sum(earlier * counts[None, :], axis=1)
    slot_local = jnp.arange(slot_size, dtype=jnp.int32)[None, :]
    keep = (slot_local < counts[:, None]) & (base[:, None] + slot_local < copy_room_sizes[me])
    result = expert_mlp(
        arrived.reshape(slot_total, width), first_layer_matrix[0], second_layer_matrix[0]
    )
    kept = jnp.where(keep.reshape(-1, 1), result, 0.0).astype(jnp.bfloat16)
    returned = lax.all_to_all(
        kept.reshape(experts, slot_size, width), "expert", split_axis=0, concat_axis=0, tiled=True
    ).reshape(slot_total, width)

    gate_float = whole_number_mixing_factors.astype(jnp.float32)
    gate_share = gate_float / jnp.sum(gate_float, axis=1, keepdims=True)
    task_out = pick(returned, task_slots)
    shared_out = pick(returned, shared_slots)
    return (gate_share[:, :1] * task_out + gate_share[:, 1:] * shared_out).astype(jnp.bfloat16)


def solution(mesh):
    in_specs = (
        P(("groups", "expert"), None),
        P(("groups", "expert")),
        P(("groups", "expert"), None),
        P(("groups", "expert"), None),
        P(),
        P("expert", None, None),
        P("expert", None, None),
    )
    out_specs = P(("groups", "expert"), None)
    return jax.shard_map(shards, mesh=mesh, in_specs=in_specs, out_specs=out_specs, check_vma=False)
```

time: 77.9 us -> 76.6 us (0.983); the launches traced: 77.3 us -> 75.1 us
  waiting for transfers between devices: 29 us -> 44.5 us
  starting transfers between devices: 22.9 us -> 14.2 us
  matrix products: 18.1 us -> 11.9 us
  other arithmetic: 3.7 us -> 2.39 us
  between operations: 1.32 us -> 0.11 us
    all_to_all x5 -> x2, waiting for transfers between devices: 19.1 us -> 44.5 us  [the longest x1 22.8 us: shards(): lax.all_to_all(kept.reshape(experts, slot_size, width), 'expert', split_a...]
    ppermute x3 -> x0, waiting for transfers between devices: 9.89 us -> none  [the longest x1 7.75 us: shards(): guest_rows = lax.ppermute(query_features, 'expert', swap)]
    ppermute x3 -> x0, starting transfers between devices: 4.84 us -> none  [the longest x1 4.06 us: shards(): guest_id = lax.ppermute(far_id, 'expert', swap)]
    dot_general x2 -> x1, matrix products: 13.7 us -> 9.07 us  [expert_mlp(): return jnp.dot(hidden, down_matrix, preferred_element_type=jnp.float32)]
    all_to_all x5 -> x2, starting transfers between devices: 18.1 us -> 14.2 us  [the longest x1 7.41 us: shards(): lax.all_to_all(sent.reshape(experts, slot_size, width), 'expert', split_a...]
    dot_general x2 -> x1, matrix products: 3.13 us -> 1.42 us  [shards(): jnp.dot(place.astype(jnp.bfloat16), query_features, preferred_element_typ...]
    lt x2 -> x0, other arithmetic: 1.53 us -> none  [serve(): keep = (base[:, None] + slot_local[None, :] < room).reshape(-1, 1)]
  transfers between devices with their start and end apart: 8 -> 2, of which waited for: 6 -> 2; matrix products, arithmetic and copies ran while one was open for 29% -> 2% of each run, Pallas kernels for 0% -> 0%
where the time goes in v4:
time: 76.6 us; the launch traced here: 75.1 us
  waiting for transfers between devices  44.5 us (58%)
  starting transfers between devices  14.2 us (19%)
  matrix products  11.9 us (16%)
  other arithmetic  2.39 us (3%)
  local copies, waits for them, and re-layouts  2.07 us (3%)
    all_to_all x1, waiting for transfers between devices, shards(): lax.all_to_all(kept.reshape(experts, slot_size, width), 'expert', split_a...  22.8 us
    all_to_all x1, waiting for transfers between devices, shards(): lax.all_to_all(sent.reshape(experts, slot_size, width), 'expert', split_a...  21.6 us
    dot_general x1, matrix products, expert_mlp(): return jnp.dot(hidden, down_matrix, preferred_element_type=jnp.float32)  9.07 us
    all_to_all x1, starting transfers between devices, shards(): lax.all_to_all(sent.reshape(experts, slot_size, width), 'expert', split_a...  7.41 us
    all_to_all x1, starting transfers between devices, shards(): lax.all_to_all(kept.reshape(experts, slot_size, width), 'expert', split_a...  6.79 us
  transfers between devices with their start and end apart: 2, of which 2 were waited for; matrix products, arithmetic and copies ran while one was open for 2% of the time, Pallas kernels for 0%

profile of v4, /device:TPU:0, one launch (start us, length us, event | category | flops | bytes accessed | tf_op | source)
XLA Modules:
  0.0 75.1 jit_solution(15028828388539756602)
XLA Ops:
  0.0 0.0 copy-start
  0.0 0.7 slice_bitcast_fusion.2
  0.7 0.2 convert_reduce_fusion.1
  0.9 0.8 %fusion.30 = (s32[128]{0:T(128)S(1)}, s32[128]{0:T(128)S(1)}) fusion(s32[128,2]{0,1:T(2,128)} %param.9, s32[128]{0:T(128)} %param.8, s32[128]{0:T(128)S(1)} %convert_reduce_fusion.1), kind=kLoop, calls=%fused_computation.48 | loop fusion | flops 640 | bytes 3072 | tf_op jit(solution)/shard_map/sub | solution.py:49
  1.7 0.2 convert_reduce_fusion.2
  1.9 0.1 convert_reduce_fusion
  2.0 0.0 copy-done
  2.0 1.4 %add_convert_fusion = bf16[512,1024]{1,0:T(8,128)(2,1)} fusion(bf16[128,1024]{1,0:T(8,128)(2,1)S(1)} %copy-done, f32[512]{0:T(512)S(1)} %multiply_subtract_fusion, s32[128]{0:T(128)S(1)} %get-tuple-element.8, s32[128]{0:T(128)S(1)} %multiply_add_fusion.1), kind=kOutput, calls=%fused_computation.14 | convolution fusion | flops 135462912 | bytes 1313792 | tf_op jit(solution)/shard_map/dot_general | solution.py:58
  3.4 7.4 %all-to-all-start = ((bf16[16,32,1024]{2,1,0:T(8,128)(2,1)}), bf16[16,32,1024]{2,1,0:T(8,128)(2,1)S(1)}, u32[]{:S(2)}, u32[]{:S(2)}) async-start(bf16[16,32,1024]{2,1,0:T(8,128)(2,1)} %bitcast.3), calls=%async_computation | async-start | bytes 2097152 | tf_op jit(solution)/shard_map/all_to_all | solution.py:60
  10.9 1.2 %dynamic_slice.3 = s32[1]{0:T(128)} dynamic-slice(s32[16]{0:T(128)} %param.11, s32[]{:T(128)S(6)} %select_n.20), dynamic_slice_sizes={1} | dynamic-slice | bytes 12 | tf_op jit(solution)/shard_map/dynamic_slice | solution.py:72
  12.1 21.6 %all-to-all-done = bf16[16,32,1024]{2,1,0:T(8,128)(2,1)S(1)} async-done(((bf16[16,32,1024]{2,1,0:T(8,128)(2,1)}), bf16[16,32,1024]{2,1,0:T(8,128)(2,1)S(1)}, u32[]{:S(2)}, u32[]{:S(2)}) %all-to-all-start) | async-done | bytes 1048608 | tf_op jit(solution)/shard_map/all_to_all | solution.py:60
  33.7 0.1 slice_reduce_fusion
  33.9 0.1 convert_reduce_fusion.3
  34.0 0.1 select_reduce_fusion
  34.1 0.7 fusion.28
  34.9 0.1 and.31
  34.9 0.0 copy-start.2
  35.0 9.1 %select_convert_fusion = bf16[512,1024]{1,0:T(8,128)(2,1)} fusion(bf16[1,2048,1024]{2,1,0:T(8,128)(2,1)} %param.13, pred[512]{0:T(512)(128)(4,1)S(1)} %and.31, bf16[512,1024]{1,0:T(8,128)(2,1)S(1)} %bitcast.41, bf16[1,1024,2048]{2,1,0:T(8,128)(2,1)} %param.12), kind=kOutput, calls=%fused_computation.13 | convolution fusion | flops 4305453056 | bytes 10486272 | tf_op jit(solution)/shard_map/dot_general | solution.py:14
  44.0 6.8 %all-to-all-start.1 = ((bf16[16,32,1024]{2,1,0:T(8,128)(2,1)}), bf16[16,32,1024]{2,1,0:T(8,128)(2,1)S(1)}, u32[]{:S(2)}, u32[]{:S(2)}) async-start(bf16[16,32,1024]{2,1,0:T(8,128)(2,1)} %bitcast.8), calls=%async_computation.1 | async-start | bytes 2097152 | tf_op jit(solution)/shard_map/all_to_all | solution.py:77
  50.8 0.0 copy-done.2
  50.9 0.0 copy-done.1
  50.9 22.8 %all-to-all-done.1 = bf16[16,32,1024]{2,1,0:T(8,128)(2,1)S(1)} async-done(((bf16[16,32,1024]{2,1,0:T(8,128)(2,1)}), bf16[16,32,1024]{2,1,0:T(8,128)(2,1)S(1)}, u32[]{:S(2)}, u32[]{:S(2)}) %all-to-all-start.1) | async-done | bytes 1048608 | tf_op jit(solution)/shard_map/all_to_all | solution.py:77
  73.7 0.4 convolution_multiply_fusion.1
  74.1 1.1 %fusion.17 = bf16[128,1024]{1,0:T(8,128)(2,1)} fusion(f32[128,1024]{1,0:T(8,128)S(1)} %convolution_multiply_fusion.1, bf16[512,1024]{1,0:T(8,128)(2,1)S(1)} %bitcast.40, f32[128]{0:T(128)S(1)} %get-tuple-element.5, s32[128]{0:T(128)S(1)} %fusion.29), kind=kOutput, calls=%fused_computation.18 | convolution fusion | flops 134676480 | bytes 1836032 | tf_op jit(solution)/shard_map/dot_general | solution.py:29
  (7 shorter events, 0.0 us)
Async XLA Ops:
  0.0 2.0 %copy-start = (bf16[128,1024]{1,0:T(8,128)(2,1)S(1)}, bf16[128,1024]{1,0:T(8,128)(2,1)}, u32[]{:S(2)}) copy-start(bf16[128,1024]{1,0:T(8,128)(2,1)} %param.7) | copy-start | bytes 786436
  3.4 30.3 %all-to-all-start = ((bf16[16,32,1024]{2,1,0:T(8,128)(2,1)}), bf16[16,32,1024]{2,1,0:T(8,128)(2,1)S(1)}, u32[]{:S(2)}, u32[]{:S(2)}) async-start(bf16[16,32,1024]{2,1,0:T(8,128)(2,1)} %bitcast.3), calls=%async_computation | async-start | bytes 2097152 | tf_op jit(solution)/shard_map/all_to_all | solution.py:60
  34.9 15.9 %copy-start.2 = (s32[128,2]{0,1:T(2,128)S(1)}, s32[128,2]{0,1:T(2,128)}, u32[]{:S(2)}) copy-start(s32[128,2]{0,1:T(2,128)} %param.10) | copy-start | bytes 3076
  34.9 15.9 %copy-start.1 = (s32[128,2]{0,1:T(2,128)S(1)}, s32[128,2]{0,1:T(2,128)}, u32[]{:S(2)}) copy-start(s32[128,2]{0,1:T(2,128)} %param.9) | copy-start | bytes 3076
  44.0 29.7 %all-to-all-start.1 = ((bf16[16,32,1024]{2,1,0:T(8,128)(2,1)}), bf16[16,32,1024]{2,1,0:T(8,128)(2,1)S(1)}, u32[]{:S(2)}, u32[]{:S(2)}) async-start(bf16[16,32,1024]{2,1,0:T(8,128)(2,1)} %bitcast.8), calls=%async_computation.1 | async-start | bytes 2097152 | tf_op jit(solution)/shard_map/all_to_all | solution.py:77
